TPU v7x, 16 devices: a 4x2x1 block of a 4x4x8 slice. The times are simulated.
16 devices in a mesh: frag: 2 (over y, z), dev: 8 (over x, core).
Axes of the slice: x: 4, y: 2, z: 1, core: 2. Of those that a mesh axis runs over, the one named last changes fastest.
The devices are a block of a 4x4x8 slice.
Arguments:
- ao_ints: bfloat16 [272, 136, 136, 136], P(('frag', 'dev')), parts along dimension 0
- occ_coef: bfloat16 [272, 54], P('frag'), parts along dimension 0
- virt_coef: bfloat16 [272, 56], P('frag'), parts along dimension 0
Outputs:
- output: float32 [108, 56, 3024], P('frag', None, 'dev'), parts along dimension 0
There are 2 independent parts. A program takes and returns all parts, laid end to end along the dimension named above; each array names one.
All inputs are finite; a program needn't handle non-finite values.
Results may differ from a plain program's by a relative error of at most 0.001.
Values are sent between devices in bfloat16 or wider.
A program may use at most 768 MiB of HBM per device.

v0:
```python
import jax
import jax.numpy as jnp
from jax import lax
from jax.sharding import PartitionSpec as P


def solution(mesh):
    def local_part(ao_rows, occ_coef, virt_coef):
        quarter = jnp.einsum("pqrs,rj->pqsj", ao_rows, occ_coef, preferred_element_type=jnp.float32).astype(jnp.bfloat16)
        half_ints = jnp.einsum("pqsj,sb->pqjb", quarter, virt_coef, preferred_element_type=jnp.float32).astype(jnp.bfloat16)
        rows_here, ao_dim, occ_dim, virt_dim = half_ints.shape
        half_ints = half_ints.reshape(rows_here, ao_dim, occ_dim * virt_dim)
        pair_block = lax.all_to_all(half_ints, "dev", 2, 0, tiled=True)
        three_quarter = jnp.einsum("qa,pqc->apc", virt_coef, pair_block, preferred_element_type=jnp.float32).astype(jnp.bfloat16)
        return jnp.einsum("pi,apc->iac", occ_coef, three_quarter, preferred_element_type=jnp.float32)

    return jax.shard_map(
        local_part,
        mesh=mesh,
        in_specs=(P(("frag", "dev"), None, None, None), P("frag", None), P("frag", None)),
        out_specs=P("frag", None, "dev"),
        check_vma=False,
    )
```

profile of v0, /device:TPU:113, one launch (start us, length us, event | category | flops | bytes accessed | tf_op | source)
XLA Modules:
  0.0 524.8 jit_solution(15714359023256787615)
XLA Ops:
  0.0 0.0 copy-start
  0.0 0.7 copy-done
  0.7 0.0 copy-start.1
  0.8 72.2 %convolution_convert_fusion = bf16[17,136,136,54]{2,3,1,0:T(8,128)(2,1)} fusion(bf16[17,136,136,136]{3,2,1,0:T(8,128)(2,1)} %param.3, bf16[136,54]{0,1:T(8,128)(2,1)S(1)} %copy-done), kind=kOutput, calls=%fused_computation.2 | convolution fusion | flops 4635356672 | bytes 119498848 | tf_op jit(solution)/shard_map/pqrs,rj->pqsj/dot_general | solution.py:9
  73.0 0.0 copy-done.1
  73.0 40.5 %fusion.2 = bf16[17,136,54,56]{1,3,2,0:T(8,128)(2,1)} fusion(bf16[17,136,136,54]{2,3,1,0:T(8,128)(2,1)} %convolution_convert_fusion, bf16[136,56]{0,1:T(8,128)(2,1)S(1)} %copy-done.1), kind=kOutput, calls=%fused_computation.3 | convolution fusion | flops 1908676224 | bytes 47956864 | tf_op jit(solution)/shard_map/pqsj,sb->pqjb/dot_general | solution.py:10
  113.5 40.1 %copy.27 = bf16[17,136,3024]{1,0,2:T(8,128)(2,1)} copy(bf16[17,136,3024]{1,2,0:T(8,128)(2,1)} %bitcast.35) | data formatting | bytes 27965952 | tf_op jit(solution)/shard_map/reshape | solution.py:12
  153.6 75.6 %reshape.8 = bf16[8,2,436968]{2,1,0:T(2,128)(2,1)} reshape(bf16[3024,17,136]{2,1,0:T(8,128)(2,1)} %bitcast.33) | data formatting | bytes 27965952
  229.1 161.8 %all_to_all.18 = bf16[8,2,436968]{2,1,0:T(2,128)(2,1)} all-to-all(bf16[8,2,436968]{2,1,0:T(2,128)(2,1)} %reshape.8), channel_id=1, replica_groups=mesh['frag'=2,'dev'=8] {'dev'}, dimensions={0} | all-to-all | bytes 27965952 | tf_op jit(solution)/shard_map/all_to_all | solution.py:13
  391.0 81.1 %reshape.9 = bf16[3024,17,136]{2,1,0:T(8,128)(2,1)} reshape(bf16[8,2,436968]{2,1,0:T(2,128)(2,1)} %all_to_all.18) | data formatting | bytes 27965952
  472.1 41.6 %copy.11 = bf16[8,17,136,378]{3,2,1,0:T(8,128)(2,1)} copy(bf16[8,17,136,378]{2,1,3,0:T(8,128)(2,1)} %bitcast.32) | data formatting | bytes 27965952 | tf_op jit(solution)/shard_map/all_to_all | solution.py:13
  513.7 7.1 %convert_bitcast_fusion = bf16[56,136,378]{2,0,1:T(8,128)(2,1)S(1)} fusion(bf16[136,136,378]{2,1,0:T(8,128)(2,1)} %bitcast.34, bf16[136,56]{0,1:T(8,128)(2,1)S(1)} %copy-done.1), kind=kOutput, calls=%fused_computation.6 | convolution fusion | flops 785925504 | bytes 19755904 | tf_op jit(solution)/shard_map/qa,pqc->apc/dot_general | solution.py:14
  520.8 0.9 fusion.7
  521.8 3.0 copy.13
Async XLA Ops:
  0.0 0.7 copy-start
  0.7 72.3 %copy-start.1 = (bf16[136,56]{0,1:T(8,128)(2,1)S(1)}, bf16[136,56]{0,1:T(8,128)(2,1)}, u32[]{:S(2)}) copy-start(bf16[136,56]{0,1:T(8,128)(2,1)} %param.5) | copy-start | bytes 45700
where the time goes:
time: 527 us; the launch traced here: 525 us
  local copies, waits for them, and re-layouts  242 us (46%)
  blocking collectives  162 us (31%)
  matrix products  121 us (23%)
    all_to_all x1, blocking collectives, local_part(): pair_block = lax.all_to_all(half_ints, 'dev', 2, 0, tiled=True)  162 us
    unnamed x6, local copies, waits for them, and re-layouts  157 us
    dot_general x1, matrix products, local_part(): jnp.einsum('pqrs,rj->pqsj', ao_rows, occ_coef, preferred_element_type=jnp...  72.2 us
    all_to_all x1, local copies, waits for them, and re-layouts, local_part(): pair_block = lax.all_to_all(half_ints, 'dev', 2, 0, tiled=True)  41.6 us
    dot_general x1, matrix products, local_part(): jnp.einsum('pqsj,sb->pqjb', quarter, virt_coef, preferred_element_type=jn...  40.5 us
    reshape x1, local copies, waits for them, and re-layouts, local_part(): half_ints = half_ints.reshape(rows_here, ao_dim, occ_dim * virt_dim)  40.1 us

commit v1 on v0

v1 whole, which is shorter than its diff:
```python
import functools

import jax
import jax.numpy as jnp
from jax import lax
from jax.experimental import pallas as pl
from jax.experimental.pallas import tpu as pltpu
from jax.sharding import PartitionSpec as P

LANES = 128
SUBL = 8
Q_CHUNK = 34
SLOTS = 2
SKEW = 4
HS = 137


def _up(x, m):
    return -(-x // m) * m


def _half_kernel(ndev, cblk, ao, cot, cvt, g_out, abuf, co_s, cv_s, hbuf, gbuf, asem, gsem):
    rows, n = ao.shape[0], ao.shape[1]
    occ, virt = cot.shape[0], cvt.shape[0]
    occ_p = _up(occ, SUBL)
    nch = n // Q_CHUNK
    steps = rows * nch

    co_s[...] = jnp.zeros(co_s.shape, co_s.dtype)
    co_s[0:occ, :] = cot[...]
    cv_s[...] = jnp.zeros(cv_s.shape, cv_s.dtype)
    cv_s[:, 0:virt] = cvt[...].astype(jnp.float32).T.astype(jnp.bfloat16)

    def fetch(step):
        slot = lax.rem(step, SLOTS)
        p, ch = step // nch, lax.rem(step, nch)
        return pltpu.make_async_copy(
            ao.at[p, pl.ds(ch * Q_CHUNK, Q_CHUNK)], abuf.at[slot], asem.at[slot]
        )

    for s in range(SLOTS):
        fetch(s).start()

    def put(p, slot):
        return pltpu.make_async_copy(gbuf.at[slot], g_out.at[:, p], gsem.at[slot])

    def row(p, carry):
        def chunk(ch, c):
            step = p * nch + ch
            slot = lax.rem(step, SLOTS)
            fetch(step).wait()
            def first(k):
                t = [
                    jnp.dot(co_s[...], abuf[slot, k + i], preferred_element_type=jnp.float32)
                    for i in range(2)
                ]
                return jnp.concatenate(t, axis=0).astype(jnp.bfloat16)

            def second(k, t):
                h = jnp.dot(t, cv_s[...], preferred_element_type=jnp.float32)
                for i in range(2):
                    q = ch * Q_CHUNK + k + i
                    hbuf[pl.ds(q, occ_p, stride=HS), :] = h[i * occ_p : (i + 1) * occ_p]

            pend = []
            for k in range(0, Q_CHUNK, 2):
                pend.append((k, first(k)))
                if len(pend) > SKEW:
                    second(*pend.pop(0))
            for item in pend:
                second(*item)

            @pl.when(step + SLOTS < steps)
            def _():
                fetch(step + SLOTS).start()

            return c

        lax.fori_loop(0, nch, chunk, 0)

        gslot = lax.rem(p, 2)

        @pl.when(p >= 2)
        def _():
            put(p - 2, gslot).wait()

        for j in range(0, occ, 2):
            hh = [hbuf[(j + i) * HS : (j + i) * HS + n, :] for i in range(2)]
            hh = jnp.concatenate(hh, axis=1).astype(jnp.bfloat16)
            g = jnp.dot(cvt[...], hh, preferred_element_type=jnp.float32).astype(jnp.bfloat16)
            for i in range(2):
                c0, base, left = (j + i) * virt, i * LANES, virt
                while left:
                    d, l = c0 // cblk, c0 % cblk
                    w = min(left, cblk - l)
                    gbuf[gslot, d, :, l : l + w] = g[:, base : base + w]
                    c0, base, left = c0 + w, base + w, left - w
        put(p, gslot).start()
        return carry

    lax.fori_loop(0, rows, row, 0)
    for p in (rows - 2, rows - 1):
        put(p, p % 2).wait()


def _last_kernel(g, cot, out, co_s, *bufs):
    n, na, cblk = g.shape
    occ = cot.shape[0]
    occ_p = co_s.shape[0]
    nt = len(bufs) // 2
    xs, ys = bufs[:nt], bufs[nt:]

    co_s[...] = jnp.zeros(co_s.shape, co_s.dtype)
    co_s[0:occ, :] = cot[...]
    for t in range(nt):
        w = min(LANES, cblk - t * LANES)
        xs[t][...] = g[:, :, t * LANES : t * LANES + w].astype(jnp.float32).reshape(n * na, w)
    for a in range(na):
        for t in range(nt):
            x = xs[t][pl.ds(a, n, stride=na), :].astype(jnp.bfloat16)
            y = jnp.dot(co_s[...], x, preferred_element_type=jnp.float32)
            ys[t][pl.ds(a, occ_p, stride=na), :] = y
    for t in range(nt):
        w = min(LANES, cblk - t * LANES)
        out[:, :, t * LANES : t * LANES + w] = ys[t][0 : occ * na, :].reshape(occ, na, w)


def solution(mesh):
    ndev = mesh.shape["dev"]

    def local_part(ao_rows, occ_coef, virt_coef):
        rows, n = ao_rows.shape[0], ao_rows.shape[1]
        occ, virt = occ_coef.shape[1], virt_coef.shape[1]
        occ_p = _up(occ, SUBL)
        cblk = occ * virt // ndev
        cot, cvt = occ_coef.T, virt_coef.T

        g = pl.pallas_call(
            functools.partial(_half_kernel, ndev, cblk),
            out_shape=jax.ShapeDtypeStruct((ndev, rows, virt, cblk), jnp.bfloat16),
            in_specs=[
                pl.BlockSpec(memory_space=pl.ANY),
                pl.BlockSpec(memory_space=pltpu.VMEM),
                pl.BlockSpec(memory_space=pltpu.VMEM),
            ],
            out_specs=pl.BlockSpec(memory_space=pl.ANY),
            scratch_shapes=[
                pltpu.VMEM((SLOTS, Q_CHUNK, n, n), jnp.bfloat16),
                pltpu.VMEM((occ_p, n), jnp.bfloat16),
                pltpu.VMEM((n, LANES), jnp.bfloat16),
                pltpu.VMEM((occ_p * HS, LANES), jnp.float32),
                pltpu.VMEM((2, ndev, virt, cblk), jnp.bfloat16),
                pltpu.SemaphoreType.DMA((SLOTS,)),
                pltpu.SemaphoreType.DMA((2,)),
            ],
            compiler_params=pltpu.CompilerParams(vmem_limit_bytes=48 * 2**20),
            name="first_three",
        )(ao_rows, cot, cvt)

        g = lax.all_to_all(g, "dev", 0, 0, tiled=True).reshape(ndev * rows, virt, cblk)

        a_blk = SUBL
        widths = [min(LANES, cblk - l) for l in range(0, cblk, LANES)]
        return pl.pallas_call(
            _last_kernel,
            grid=(virt // a_blk,),
            out_shape=jax.ShapeDtypeStruct((occ, virt, cblk), jnp.float32),
            in_specs=[
                pl.BlockSpec((n, a_blk, cblk), lambda k: (0, k, 0)),
                pl.BlockSpec((occ, n), lambda k: (0, 0)),
            ],
            out_specs=pl.BlockSpec((occ, a_blk, cblk), lambda k: (0, k, 0)),
            scratch_shapes=[pltpu.VMEM((occ_p, n), jnp.bfloat16)]
            + [pltpu.VMEM((n * a_blk, w), jnp.float32) for w in widths]
            + [pltpu.VMEM((occ_p * a_blk, w), jnp.float32) for w in widths],
            compiler_params=pltpu.CompilerParams(vmem_limit_bytes=32 * 2**20),
            name="last",
        )(g, cot)

    return jax.shard_map(
        local_part,
        mesh=mesh,
        in_specs=(P(("frag", "dev"), None, None, None), P("frag", None), P("frag", None)),
        out_specs=P("frag", None, "dev"),
        check_vma=False,
    )
```

time: 527 us -> 164 us (0.31)
  local copies, waits for them, and re-layouts: 242 us -> 1.49 us
  matrix products: 121 us -> 0 us
  blocking collectives: 162 us -> 72.4 us
  Pallas kernels: 0 us -> 89.4 us
    unnamed x6 -> x4, local copies, waits for them, and re-layouts: 157 us -> 1.49 us
    dot_general x4 -> x0, matrix products: 121 us -> none  [the longest x1 72.2 us: local_part(): jnp.einsum('pqrs,rj->pqsj', ao_rows, occ_coef, preferred_element_type=jnp...]
    pallas_call x0 -> x2, Pallas kernels: none -> 89.4 us  [the longest x1 82.8 us: local_part(): pl.pallas_call(functools.partial(_half_kernel, ndev, cblk), out_shape=jax...]
    all_to_all x1, blocking collectives: 162 us -> 72.4 us  [local_part(): lax.all_to_all(g, 'dev', 0, 0, tiled=True).reshape(ndev * rows, virt, cblk)]
    all_to_all x1 -> x0, local copies, waits for them, and re-layouts: 41.6 us -> none  [local_part(): pair_block = lax.all_to_all(half_ints, 'dev', 2, 0, tiled=True)]
    reshape x1 -> x0, local copies, waits for them, and re-layouts: 40.1 us -> none  [local_part(): half_ints = half_ints.reshape(rows_here, ao_dim, occ_dim * virt_dim)]
where the time goes in v1:
time: 164 us; the launch traced here: 163 us
  Pallas kernels  89.4 us (55%)
  blocking collectives  72.4 us (44%)
    pallas_call x1, Pallas kernels, local_part(): pl.pallas_call(functools.partial(_half_kernel, ndev, cblk), out_shape=jax...  82.8 us
    all_to_all x1, blocking collectives, local_part(): lax.all_to_all(g, 'dev', 0, 0, tiled=True).reshape(ndev * rows, virt, cblk)  72.4 us
    pallas_call x1, Pallas kernels, local_part(): pl.pallas_call(_last_kernel, grid=(virt // a_blk,), out_shape=jax.ShapeDt...  6.58 us

profile of v1, /device:TPU:113, one launch (start us, length us, event | category | flops | bytes accessed | tf_op | source)
XLA Modules:
  0.0 163.4 jit_solution(12793473475351075863)
XLA Ops:
  0.0 0.0 copy-start
  0.0 0.7 copy-done
  0.7 0.0 copy-start.1
  0.8 0.7 copy-done.1
  1.5 82.8 %first_three.1 = bf16[8,17,56,378]{3,2,1,0:T(8,128)(2,1)S(1)} custom-call(bf16[17,136,136,136]{3,2,1,0:T(8,128)(2,1)} %ao.1, bf16[54,136]{1,0:T(8,128)(2,1)S(1)} %bitcast.4, bf16[56,136]{1,0:T(8,128)(2,1)S(1)} %bitcast.6), custom_call_target="tpu_custom_call" | custom-call | tf_op jit(solution)/shard_map/first_three/pallas_call | solution.py:138
  84.3 72.4 %all_to_all.5 = bf16[8,17,56,378]{3,2,1,0:T(8,128)(2,1)S(1)} all-to-all(bf16[8,17,56,378]{3,2,1,0:T(8,128)(2,1)S(1)} %first_three.1), channel_id=1, replica_groups=mesh['frag'=2,'dev'=8] {'dev'}, dimensions={0} | all-to-all | bytes 11515392 | tf_op jit(solution)/shard_map/all_to_all | solution.py:160
  156.8 6.6 %last.1 = f32[54,56,378]{2,1,0:T(8,128)} custom-call(bf16[136,56,378]{2,1,0:T(8,128)(2,1)S(1)} %bitcast.3, bf16[54,136]{1,0:T(8,128)(2,1)S(1)} %bitcast.5), custom_call_target="tpu_custom_call" | custom-call | tf_op jit(solution)/shard_map/last/pallas_call | solution.py:164
Async XLA Ops:
  0.0 0.7 copy-start
  0.7 0.7 copy-start.1
